TPU v7x, 32 devices: a whole 2x2x4 slice. The times are simulated.
32 devices in a mesh: gx: 4 (over z), gy: 4 (over y, x), gz: 2 (over core).
Axes of the slice: x: 2, y: 2, z: 4, core: 2. Of those that a mesh axis runs over, the one named last changes fastest.
Arguments:
- positions: float32 [3, 64, 64, 512], P(None, 'gx', 'gy', 'gz'), may hold values from -6 to 6
- pair_node: int32 [4, 4, 2, 32, 256], P('gx', 'gy', 'gz'), may hold values from 0 to 255
- pair_line: int32 [4, 4, 2, 32], P('gx', 'gy', 'gz'), may hold values from 0 to 255
- pair_far: int32 [4, 4, 2, 32, 256], P('gx', 'gy', 'gz'), may hold values from 0 to 261, as said below
- far_line: int32 [4, 4, 2, 32], P('gx', 'gy', 'gz'), may hold values from 0 to 483, as said below
- pair_geom: float32 [4, 4, 2, 32, 4, 256], P('gx', 'gy', 'gz'), may hold values from -4 to 4
- live_blocks: int32 [4, 4, 2], P('gx', 'gy', 'gz'), may hold values from 8 to 32, as said below
Outputs:
- corrected: float32 [3, 64, 64, 512], P(None, 'gx', 'gy', 'gz')
- sweep_history: float32 [2, 5], replicated
Inputs may be any that keep to these rules, and one draw needn't show every extreme that they name: `pair_far`: together with far_line: at most one of the three coordinates of node b lies outside the owner block's own nodes; node b lies inside the whole grid; in slots below 16 node b is one of the owner block's own nodes. `far_line`: together with pair_far, as stated there. `live_blocks`: some owner block has all 32 slots live.
All inputs are finite; a program needn't handle non-finite values.
Results may differ from a plain program's by a relative error of at most 0.0001.
Values sent between devices are 32-bit elements; how exact they have to be, the bound alone decides.
A program may use at most 64 MiB of HBM per device.

v0:
```python
import math
import jax
import jax.numpy as jnp
from jax import lax
from jax.sharding import PartitionSpec as P

RIM = 3
SWEEPS = 5
relax_factor = 0.9
highest = lax.Precision.HIGHEST


def extended(cells, sides, width):
    for axis, dim in sides:
        count = lax.axis_size(axis)
        ends = count - 1
        head = lax.slice_in_dim(cells, 0, width, axis=dim)
        tail = lax.slice_in_dim(cells, cells.shape[dim] - width, cells.shape[dim], axis=dim)
        cells = jnp.concatenate(
            [
                lax.ppermute(tail, axis, [(i, (i + 1) % count) for i in range(ends)]),
                cells,
                lax.ppermute(head, axis, [((i + 1) % count, i) for i in range(ends)]),
            ],
            axis=dim,
        )
    return cells


def node_sums(contribs, within, line_index, line_length, count_lines):
    blocks = contribs.shape[0]
    group_size = math.gcd(16, blocks)
    row_count = contribs.shape[1]
    columns = lax.broadcasted_iota(jnp.int32, (1, 1, line_length), 2)
    line_ids = lax.broadcasted_iota(jnp.int32, (1, count_lines), 1)

    def node_add_group(turn_idx, running):
        first_block = turn_idx * group_size
        term_part = lax.dynamic_slice_in_dim(contribs, first_block, group_size, 0)
        node_part = lax.dynamic_slice_in_dim(within, first_block, group_size, 0)
        line_part = lax.dynamic_slice_in_dim(line_index, first_block, group_size, 0)
        one_hot = (node_part[:, :, None] == columns).astype(jnp.float32)
        window = jnp.einsum("bcp,bpn->bcn", term_part, one_hot, precision=highest)
        line_hot = (line_part[:, None] == line_ids).astype(jnp.float32)
        return running + jnp.einsum("bl,bcn->cln", line_hot, window, precision=highest)

    initial = jnp.zeros((row_count, count_lines, line_length), jnp.float32)
    return lax.fori_loop(0, blocks // group_size, node_add_group, initial)


def select_lines(line_hot, field_lines):
    return jnp.einsum("bl,cln->bcn", line_hot, field_lines, precision=highest)


def sweep_terms(
    near_lines, far_lines, within, far_pos, line_index, geometry, live_mask, count_lines
):
    blocks = within.shape[0]
    group_size = math.gcd(16, blocks)
    near_cols = lax.broadcasted_iota(jnp.int32, (1, 1, near_lines.shape[2]), 2)
    far_cols = lax.broadcasted_iota(jnp.int32, (1, 1, far_lines.shape[2]), 2)
    line_ids = lax.broadcasted_iota(jnp.int32, (1, count_lines), 1)

    def sweep_add_group(turn_idx, carry):
        running, energy_sum = carry
        near_hot = (within[:, :, None] == near_cols).astype(jnp.float32)
        far_hot = (far_pos[:, :, None] == far_cols).astype(jnp.float32)
        near_vals = jnp.einsum("bcn,bpn->bcp", near_lines, near_hot, precision=highest)
        far_vals = jnp.einsum("bcn,bpn->bcp", far_lines, far_hot, precision=highest)
        differ = near_vals - far_vals
        gap_value = (
            geometry[:, 0, :] * differ[:, 0, :]
            + geometry[:, 1, :] * differ[:, 1, :]
            + geometry[:, 2, :] * differ[:, 2, :]
            - geometry[:, 3, :]
        )
        depth_value = jnp.where(live_mask, jnp.maximum(-gap_value, 0.0), 0.0)
        contribs = depth_value[:, None, :] * geometry[:, 0:3, :]
        window = jnp.einsum("bcp,bpn->bcn", contribs, near_hot, precision=highest)
        line_hot = (line_index[:, None] == line_ids).astype(jnp.float32)
        running = running + jnp.einsum("bl,bcn->cln", line_hot, window, precision=highest)
        return (running, energy_sum + jnp.sum(depth_value * depth_value))

    initial = (
        jnp.zeros((3, count_lines, near_lines.shape[2]), jnp.float32),
        jnp.zeros((), jnp.float32),
    )
    return lax.fori_loop(0, blocks // group_size, sweep_add_group, initial)


def local(positions, pair_node, pair_line, pair_far, far_line, pair_geom, live_blocks):
    within = pair_node[0, 0, 0]
    line_index = pair_line[0, 0, 0]
    far_pos = pair_far[0, 0, 0]
    far_index = far_line[0, 0, 0]
    geometry = pair_geom[0, 0, 0]
    live_count = live_blocks[0, 0, 0]
    size_x = positions.shape[1]
    size_y = positions.shape[2]
    size_z = positions.shape[3]
    blocks = within.shape[0]
    pair_count = within.shape[1]
    inner_count = blocks // 2
    count_lines = size_x * size_y
    ext_lines = (size_x + 2 * RIM) * (size_y + 2 * RIM)
    ext_z = size_z + 2 * RIM
    devices = lax.axis_size("gx") * lax.axis_size("gy") * lax.axis_size("gz")
    slot_count = blocks * pair_count
    live_mask = lax.broadcasted_iota(jnp.int32, (blocks, 1), 0) < live_count
    near_hot = (line_index[:, None] == lax.broadcasted_iota(jnp.int32, (1, count_lines), 1)).astype(
        jnp.float32
    )
    far_hot = (far_index[:, None] == lax.broadcasted_iota(jnp.int32, (1, ext_lines), 1)).astype(
        jnp.float32
    )
    live_ones = jnp.broadcast_to(
        jnp.where(live_mask, 1.0, 0.0).astype(jnp.float32), (blocks, pair_count)
    )
    counts = node_sums(live_ones[:, None, :], within, line_index, size_z, count_lines).reshape(
        size_x, size_y, size_z
    )
    widths = ((0, 0), (RIM, RIM), (RIM, RIM), (RIM, RIM))
    padded = extended(positions, (("gx", 1), ("gy", 2), ("gz", 3)), RIM)
    current = positions
    energies = []
    residuals = []
    for sweep_idx in range(SWEEPS):
        near_lines = select_lines(near_hot, current.reshape(3, count_lines, size_z))
        local_pad = jnp.pad(current, widths).reshape(3, ext_lines, ext_z)
        inner_far = select_lines(far_hot[:inner_count], local_pad)
        inner_total, inner_energy = sweep_terms(
            near_lines[:inner_count],
            inner_far,
            within[:inner_count],
            far_pos[:inner_count],
            line_index[:inner_count],
            geometry[:inner_count],
            live_mask[:inner_count],
            count_lines,
        )
        outer_far = select_lines(far_hot[inner_count:], padded.reshape(3, ext_lines, ext_z))
        outer_total, outer_energy = sweep_terms(
            near_lines[inner_count:],
            outer_far,
            within[inner_count:],
            far_pos[inner_count:],
            line_index[inner_count:],
            geometry[inner_count:],
            live_mask[inner_count:],
            count_lines,
        )
        node_total = inner_total + outer_total
        energy_local = inner_energy + outer_energy
        total_energy = lax.psum(energy_local, ("gx", "gy", "gz"))
        scale_factor = 1.0 / (1.0 + total_energy / (slot_count * devices))
        correction = (
            relax_factor
            * scale_factor
            * node_total.reshape(3, size_x, size_y, size_z)
            / (1.0 + counts)
        )
        current = current + correction
        residual_local = jnp.sum(correction * correction)
        residuals.append(lax.psum(residual_local, ("gx", "gy", "gz")))
        energies.append(total_energy)
        if sweep_idx + 1 < SWEEPS:
            padded = extended(current, (("gx", 1), ("gy", 2), ("gz", 3)), RIM)
    history = jnp.stack(
        [
            jnp.sqrt(1.0 + jnp.stack(energies) / slot_count),
            jnp.sqrt(1.0 + jnp.stack(residuals) / (size_x * size_y * size_z)),
        ]
    )
    return (current, history)


def solution(mesh):
    return jax.shard_map(
        local,
        mesh=mesh,
        in_specs=(
            P(None, "gx", "gy", "gz"),
            P("gx", "gy", "gz", None, None),
            P("gx", "gy", "gz", None),
            P("gx", "gy", "gz", None, None),
            P("gx", "gy", "gz", None),
            P("gx", "gy", "gz", None, None, None),
            P("gx", "gy", "gz"),
        ),
        out_specs=(P(None, "gx", "gy", "gz"), P()),
        check_vma=False,
    )
```

profile of v0, /device:TPU:0, one launch (start us, length us, event | category | flops | bytes accessed | tf_op | source)
XLA Modules:
  0.0 585.4 jit_solution(6506297491511349636)
XLA Ops:
  3.7 5.6 collective-permute-start
  26.3 4.3 while.9
  33.4 4.6 collective-permute-start.2
  46.5 4.1 collective-permute-start.4
  66.3 44.0 %psum.70 = f32[]{:T(128)} all-reduce(f32[]{:T(128)S(6)} %add.349), channel_id=1, replica_groups=mesh['gx'=4,'gy'=4,'gz'=2] {'gx','gy','gz'}, use_global_device_ids=true, to_apply=%region_2.3 | all-reduce | flops 1 | bytes 8 | tf_op jit(solution)/shard_map/psum | solution.py:154
  114.8 4.6 collective-permute-start.6
  123.5 4.8 collective-permute-start.8
  138.4 3.8 collective-permute-start.10
  147.7 5.1 pad_maximum_fusion.1
  171.9 43.0 %psum.71 = f32[]{:T(128)} all-reduce(f32[]{:T(128)S(6)} %add.359), channel_id=1, replica_groups=mesh['gx'=4,'gy'=4,'gz'=2] {'gx','gy','gz'}, use_global_device_ids=true, to_apply=%region_7.8 | all-reduce | flops 1 | bytes 8 | tf_op jit(solution)/shard_map/psum | solution.py:154
  219.3 5.0 collective-permute-start.12
  228.0 4.8 collective-permute-start.14
  251.6 5.0 pad_maximum_fusion.2
  276.5 44.2 %psum.72 = f32[]{:T(128)} all-reduce(f32[]{:T(128)S(6)} %add.367), channel_id=1, replica_groups=mesh['gx'=4,'gy'=4,'gz'=2] {'gx','gy','gz'}, use_global_device_ids=true, to_apply=%region_10.11 | all-reduce | flops 1 | bytes 8 | tf_op jit(solution)/shard_map/psum | solution.py:154
  325.2 4.7 collective-permute-start.18
  333.9 4.8 collective-permute-start.20
  348.6 3.7 collective-permute-start.22
  357.8 5.1 pad_maximum_fusion.3
  382.0 43.2 %psum.73 = f32[]{:T(128)} all-reduce(f32[]{:T(128)S(6)} %add.375), channel_id=1, replica_groups=mesh['gx'=4,'gy'=4,'gz'=2] {'gx','gy','gz'}, use_global_device_ids=true, to_apply=%region_13.14 | all-reduce | flops 1 | bytes 8 | tf_op jit(solution)/shard_map/psum | solution.py:154
  429.6 4.8 collective-permute-start.24
  438.3 4.8 collective-permute-start.26
  461.8 5.0 pad_maximum_fusion.4
  490.1 44.1 %psum.74 = f32[]{:T(128)} all-reduce(f32[]{:T(128)S(6)} %add.383), channel_id=1, replica_groups=mesh['gx'=4,'gy'=4,'gz'=2] {'gx','gy','gz'}, use_global_device_ids=true, to_apply=%region_16.17 | all-reduce | flops 1 | bytes 8 | tf_op jit(solution)/shard_map/psum | solution.py:154
  539.1 39.2 %all-reduce.5 = (f32[1,1]{1,0:T(1,128)}, f32[1,1]{1,0:T(1,128)}, f32[1,1]{1,0:T(1,128)}, f32[1,1]{1,0:T(1,128)}, f32[1,1]{1,0:T(1,128)}) all-reduce(f32[1,1]{1,0:T(1,128)} %bitcast.57, f32[1,1]{1,0:T(1,128)} %bitcast.58, f32[1,1]{1,0:T(1,128)} %bitcast.59, ...), channel_id=1, replica_groups=mesh['gx'=4,'gy'=4,'gz'=2] {'gx','gy','gz'}, use_global_device_ids=true, to_apply=%region_18.19 | all-reduce | flops 5 | bytes 40 | tf_op jit(solution)/shard_map/psum | solution.py:164
  (402 shorter events, 235.3 us)
Async XLA Ops:
  2.4 29.6 %collective-permute-start.1 = (f32[3,3,16,256]{3,1,2,0:T(4,128)S(1)}, f32[3,3,16,256]{3,1,2,0:T(4,128)S(1)}, u32[]{:S(2)}, u32[]{:S(2)}) collective-permute-start(f32[3,3,16,256]{3,1,2,0:T(4,128)S(1)} %get-tuple-element.616), channel_id=1, source_target_pairs={{8,0},{16,8},{24,16},{9,1},{17,9},{25,17},{10,2},{18,10},{26,18},{... | collective-permute-start | bytes 442376 | tf_op jit(solution)/shard_map/ppermute | solution.py:23
  3.7 28.3 %collective-permute-start = (f32[3,3,16,256]{3,1,2,0:T(4,128)S(1)}, f32[3,3,16,256]{3,1,2,0:T(4,128)S(1)}, u32[]{:S(2)}, u32[]{:S(2)}) collective-permute-start(f32[3,3,16,256]{3,1,2,0:T(4,128)S(1)} %get-tuple-element.615), channel_id=1, source_target_pairs={{0,8},{8,16},{16,24},{1,9},{9,17},{17,25},{2,10},{10,18},{18,26},{... | collective-permute-start | bytes 442376 | tf_op jit(solution)/shard_map/ppermute | solution.py:21
  32.1 9.3 %collective-permute-start.3 = (f32[3,22,3,256]{3,1,2,0:T(8,128)S(1)}, f32[3,22,3,256]{3,1,2,0:T(8,128)S(1)}, u32[]{:S(2)}, u32[]{:S(2)}) collective-permute-start(f32[3,22,3,256]{3,1,2,0:T(8,128)S(1)} %get-tuple-element.590), channel_id=1, source_target_pairs={{2,0},{4,2},{6,4},{3,1},{5,3},{7,5},{10,8},{12,10},{14,12},{11,9},... | collective-permute-start | bytes 608264 | tf_op jit(solution)/shard_map/ppermute | solution.py:23
  33.4 8.7 %collective-permute-start.2 = (f32[3,22,3,256]{3,1,2,0:T(8,128)S(1)}, f32[3,22,3,256]{3,1,2,0:T(8,128)S(1)}, u32[]{:S(2)}, u32[]{:S(2)}) collective-permute-start(f32[3,22,3,256]{3,1,2,0:T(8,128)S(1)} %get-tuple-element.589), channel_id=1, source_target_pairs={{0,2},{2,4},{4,6},{1,3},{3,5},{5,7},{8,10},{10,12},{12,14},{9,11},... | collective-permute-start | bytes 608264 | tf_op jit(solution)/shard_map/ppermute | solution.py:21
  44.5 8.3 %collective-permute-start.5 = (f32[3,22,22,3]{2,1,3,0:T(8,128)}, f32[3,22,22,3]{2,1,3,0:T(8,128)S(1)}, u32[]{:S(2)}, u32[]{:S(2)}) collective-permute-start(f32[3,22,22,3]{2,1,3,0:T(8,128)} %copy.270), channel_id=1, source_target_pairs={{1,0},{3,2},{5,4},{7,6},{9,8},{11,10},{13,12},{15,14},{17,16},{19,... | collective-permute-start | bytes 52280 | tf_op jit(solution)/shard_map/ppermute | solution.py:23
  114.8 7.2 %collective-permute-start.6 = (f32[3,3,16,256]{3,2,1,0:T(8,128)S(1)}, f32[3,3,16,256]{3,2,1,0:T(8,128)S(1)}, u32[]{:S(2)}, u32[]{:S(2)}) collective-permute-start(f32[3,3,16,256]{3,2,1,0:T(8,128)S(1)} %get-tuple-element.613), channel_id=1, source_target_pairs={{0,8},{8,16},{16,24},{1,9},{9,17},{17,25},{2,10},{10,18},{18,26},{... | collective-permute-start | bytes 442376 | tf_op jit(solution)/shard_map/ppermute | solution.py:21
  122.1 9.7 %collective-permute-start.9 = (f32[3,22,3,256]{3,1,2,0:T(8,128)S(1)}, f32[3,22,3,256]{3,1,2,0:T(8,128)S(1)}, u32[]{:S(2)}, u32[]{:S(2)}) collective-permute-start(f32[3,22,3,256]{3,1,2,0:T(8,128)S(1)} %copy.294), channel_id=1, source_target_pairs={{2,0},{4,2},{6,4},{3,1},{5,3},{7,5},{10,8},{12,10},{14,12},{11,9},... | collective-permute-start | bytes 608264 | tf_op jit(solution)/shard_map/ppermute | solution.py:23
  123.5 8.4 %collective-permute-start.8 = (f32[3,22,3,256]{3,1,2,0:T(8,128)S(1)}, f32[3,22,3,256]{3,1,2,0:T(8,128)S(1)}, u32[]{:S(2)}, u32[]{:S(2)}) collective-permute-start(f32[3,22,3,256]{3,1,2,0:T(8,128)S(1)} %copy.293), channel_id=1, source_target_pairs={{0,2},{2,4},{4,6},{1,3},{3,5},{5,7},{8,10},{10,12},{12,14},{9,11},... | collective-permute-start | bytes 608264 | tf_op jit(solution)/shard_map/ppermute | solution.py:21
  135.4 10.4 %collective-permute-start.11 = (f32[3,22,22,3]{2,1,3,0:T(8,128)S(1)}, f32[3,22,22,3]{2,1,3,0:T(8,128)S(1)}, u32[]{:S(2)}, u32[]{:S(2)}) collective-permute-start(f32[3,22,22,3]{2,1,3,0:T(8,128)S(1)} %copy.298), channel_id=1, source_target_pairs={{1,0},{3,2},{5,4},{7,6},{9,8},{11,10},{13,12},{15,14},{17,16},{19,... | collective-permute-start | bytes 52280 | tf_op jit(solution)/shard_map/ppermute | solution.py:23
  138.4 7.9 %collective-permute-start.10 = (f32[3,22,22,3]{2,1,3,0:T(8,128)S(1)}, f32[3,22,22,3]{2,1,3,0:T(8,128)}, u32[]{:S(2)}, u32[]{:S(2)}) collective-permute-start(f32[3,22,22,3]{2,1,3,0:T(8,128)S(1)} %copy.297), channel_id=1, source_target_pairs={{0,1},{2,3},{4,5},{6,7},{8,9},{10,11},{12,13},{14,15},{16,17},{18,... | collective-permute-start | bytes 52280 | tf_op jit(solution)/shard_map/ppermute | solution.py:21
  218.0 7.3 %collective-permute-start.13 = (f32[3,3,16,256]{3,2,1,0:T(8,128)S(1)}, f32[3,3,16,256]{3,2,1,0:T(8,128)S(1)}, u32[]{:S(2)}, u32[]{:S(2)}) collective-permute-start(f32[3,3,16,256]{3,2,1,0:T(8,128)S(1)} %get-tuple-element.610), channel_id=1, source_target_pairs={{8,0},{16,8},{24,16},{9,1},{17,9},{25,17},{10,2},{18,10},{26,18},{... | collective-permute-start | bytes 442376 | tf_op jit(solution)/shard_map/ppermute | solution.py:23
  219.3 7.2 %collective-permute-start.12 = (f32[3,3,16,256]{3,2,1,0:T(8,128)S(1)}, f32[3,3,16,256]{3,2,1,0:T(8,128)S(1)}, u32[]{:S(2)}, u32[]{:S(2)}) collective-permute-start(f32[3,3,16,256]{3,2,1,0:T(8,128)S(1)} %get-tuple-element.609), channel_id=1, source_target_pairs={{0,8},{8,16},{16,24},{1,9},{9,17},{17,25},{2,10},{10,18},{18,26},{... | collective-permute-start | bytes 442376 | tf_op jit(solution)/shard_map/ppermute | solution.py:21
  226.7 9.0 %collective-permute-start.15 = (f32[3,22,3,256]{3,1,2,0:T(8,128)S(1)}, f32[3,22,3,256]{3,1,2,0:T(8,128)S(1)}, u32[]{:S(2)}, u32[]{:S(2)}) collective-permute-start(f32[3,22,3,256]{3,1,2,0:T(8,128)S(1)} %copy.320), channel_id=1, source_target_pairs={{2,0},{4,2},{6,4},{3,1},{5,3},{7,5},{10,8},{12,10},{14,12},{11,9},... | collective-permute-start | bytes 608264 | tf_op jit(solution)/shard_map/ppermute | solution.py:23
  228.0 8.3 %collective-permute-start.14 = (f32[3,22,3,256]{3,1,2,0:T(8,128)S(1)}, f32[3,22,3,256]{3,1,2,0:T(8,128)S(1)}, u32[]{:S(2)}, u32[]{:S(2)}) collective-permute-start(f32[3,22,3,256]{3,1,2,0:T(8,128)S(1)} %copy.319), channel_id=1, source_target_pairs={{0,2},{2,4},{4,6},{1,3},{3,5},{5,7},{8,10},{10,12},{12,14},{9,11},... | collective-permute-start | bytes 608264 | tf_op jit(solution)/shard_map/ppermute | solution.py:21
  240.3 8.5 %collective-permute-start.17 = (f32[3,22,22,3]{2,1,3,0:T(8,128)S(1)}, f32[3,22,22,3]{2,1,3,0:T(8,128)S(1)}, u32[]{:S(2)}, u32[]{:S(2)}) collective-permute-start(f32[3,22,22,3]{2,1,3,0:T(8,128)S(1)} %copy.324), channel_id=1, source_target_pairs={{1,0},{3,2},{5,4},{7,6},{9,8},{11,10},{13,12},{15,14},{17,16},{19,... | collective-permute-start | bytes 52280 | tf_op jit(solution)/shard_map/ppermute | solution.py:23
  242.1 8.0 %collective-permute-start.16 = (f32[3,22,22,3]{2,1,3,0:T(8,128)S(1)}, f32[3,22,22,3]{2,1,3,0:T(8,128)S(1)}, u32[]{:S(2)}, u32[]{:S(2)}) collective-permute-start(f32[3,22,22,3]{2,1,3,0:T(8,128)S(1)} %copy.323), channel_id=1, source_target_pairs={{0,1},{2,3},{4,5},{6,7},{8,9},{10,11},{12,13},{14,15},{16,17},{18,... | collective-permute-start | bytes 52280 | tf_op jit(solution)/shard_map/ppermute | solution.py:21
  332.5 9.5 %collective-permute-start.21 = (f32[3,22,3,256]{3,1,2,0:T(8,128)S(1)}, f32[3,22,3,256]{3,1,2,0:T(8,128)S(1)}, u32[]{:S(2)}, u32[]{:S(2)}) collective-permute-start(f32[3,22,3,256]{3,1,2,0:T(8,128)S(1)} %copy.346), channel_id=1, source_target_pairs={{2,0},{4,2},{6,4},{3,1},{5,3},{7,5},{10,8},{12,10},{14,12},{11,9},... | collective-permute-start | bytes 608264 | tf_op jit(solution)/shard_map/ppermute | solution.py:23
  333.9 8.3 %collective-permute-start.20 = (f32[3,22,3,256]{3,1,2,0:T(8,128)S(1)}, f32[3,22,3,256]{3,1,2,0:T(8,128)S(1)}, u32[]{:S(2)}, u32[]{:S(2)}) collective-permute-start(f32[3,22,3,256]{3,1,2,0:T(8,128)S(1)} %copy.345), channel_id=1, source_target_pairs={{0,2},{2,4},{4,6},{1,3},{3,5},{5,7},{8,10},{10,12},{12,14},{9,11},... | collective-permute-start | bytes 608264 | tf_op jit(solution)/shard_map/ppermute | solution.py:21
  345.7 10.2 %collective-permute-start.23 = (f32[3,22,22,3]{2,1,3,0:T(8,128)S(1)}, f32[3,22,22,3]{2,1,3,0:T(8,128)S(1)}, u32[]{:S(2)}, u32[]{:S(2)}) collective-permute-start(f32[3,22,22,3]{2,1,3,0:T(8,128)S(1)} %copy.350), channel_id=1, source_target_pairs={{1,0},{3,2},{5,4},{7,6},{9,8},{11,10},{13,12},{15,14},{17,16},{19,... | collective-permute-start | bytes 52280 | tf_op jit(solution)/shard_map/ppermute | solution.py:23
  348.6 7.8 %collective-permute-start.22 = (f32[3,22,22,3]{2,1,3,0:T(8,128)S(1)}, f32[3,22,22,3]{2,1,3,0:T(8,128)}, u32[]{:S(2)}, u32[]{:S(2)}) collective-permute-start(f32[3,22,22,3]{2,1,3,0:T(8,128)S(1)} %copy.349), channel_id=1, source_target_pairs={{0,1},{2,3},{4,5},{6,7},{8,9},{10,11},{12,13},{14,15},{16,17},{18,... | collective-permute-start | bytes 52280 | tf_op jit(solution)/shard_map/ppermute | solution.py:21
  437.0 9.0 %collective-permute-start.27 = (f32[3,22,3,256]{3,1,2,0:T(8,128)S(1)}, f32[3,22,3,256]{3,1,2,0:T(8,128)S(1)}, u32[]{:S(2)}, u32[]{:S(2)}) collective-permute-start(f32[3,22,3,256]{3,1,2,0:T(8,128)S(1)} %copy.372), channel_id=1, source_target_pairs={{2,0},{4,2},{6,4},{3,1},{5,3},{7,5},{10,8},{12,10},{14,12},{11,9},... | collective-permute-start | bytes 608264 | tf_op jit(solution)/shard_map/ppermute | solution.py:23
  438.3 8.3 %collective-permute-start.26 = (f32[3,22,3,256]{3,1,2,0:T(8,128)S(1)}, f32[3,22,3,256]{3,1,2,0:T(8,128)S(1)}, u32[]{:S(2)}, u32[]{:S(2)}) collective-permute-start(f32[3,22,3,256]{3,1,2,0:T(8,128)S(1)} %copy.371), channel_id=1, source_target_pairs={{0,2},{2,4},{4,6},{1,3},{3,5},{5,7},{8,10},{10,12},{12,14},{9,11},... | collective-permute-start | bytes 608264 | tf_op jit(solution)/shard_map/ppermute | solution.py:21
  450.6 8.5 %collective-permute-start.29 = (f32[3,22,22,3]{2,1,3,0:T(8,128)S(1)}, f32[3,22,22,3]{2,1,3,0:T(8,128)S(1)}, u32[]{:S(2)}, u32[]{:S(2)}) collective-permute-start(f32[3,22,22,3]{2,1,3,0:T(8,128)S(1)} %copy.376), channel_id=1, source_target_pairs={{1,0},{3,2},{5,4},{7,6},{9,8},{11,10},{13,12},{15,14},{17,16},{19,... | collective-permute-start | bytes 52280 | tf_op jit(solution)/shard_map/ppermute | solution.py:23
  452.4 8.0 %collective-permute-start.28 = (f32[3,22,22,3]{2,1,3,0:T(8,128)S(1)}, f32[3,22,22,3]{2,1,3,0:T(8,128)S(1)}, u32[]{:S(2)}, u32[]{:S(2)}) collective-permute-start(f32[3,22,22,3]{2,1,3,0:T(8,128)S(1)} %copy.375), channel_id=1, source_target_pairs={{0,1},{2,3},{4,5},{6,7},{8,9},{10,11},{12,13},{14,15},{16,17},{18,... | collective-permute-start | bytes 52280 | tf_op jit(solution)/shard_map/ppermute | solution.py:21
  (81 other events, 1076.8 us)
where the time goes:
time: 595 us; the launch traced here: 585 us
  blocking collectives  258 us (43%)
  matrix products  107 us (18%)
  starting transfers between devices  85.6 us (14%)
  local copies, waits for them, and re-layouts  75.5 us (13%)
  other arithmetic  37.2 us (6%)
  between operations  12.3 us (2%)
  waiting for transfers between devices  10.5 us (2%)
    psum x5, blocking collectives, local(): total_energy = lax.psum(energy_local, ('gx', 'gy', 'gz'))  218 us
    ppermute x15, starting transfers between devices, extended(): lax.ppermute(tail, axis, [(i, (i + 1) % count) for i in range(ends)])  66.1 us
    psum x1, blocking collectives, local(): residuals.append(lax.psum(residual_local, ('gx', 'gy', 'gz')))  39.2 us
    dot_general x10, matrix products, sweep_add_group(): jnp.einsum('bcn,bpn->bcp', near_lines, near_hot, precision=highest)  29.1 us
    dot_general x15, matrix products, select_lines(): return jnp.einsum('bl,cln->bcn', line_hot, field_lines, precision=highest)  27.3 us
    concatenate x10, other arithmetic, extended(): jnp.concatenate([lax.ppermute(tail, axis, [(i, (i + 1) % count) for i in...  23.8 us
    ppermute x15, starting transfers between devices, extended(): lax.ppermute(head, axis, [((i + 1) % count, i) for i in range(ends)])  19.5 us
    dot_general x10, matrix products, sweep_add_group(): far_vals = jnp.einsum('bcn,bpn->bcp', far_lines, far_hot, precision=highest)  18.4 us
  transfers between devices with their start and end apart: 30, of which 11 were waited for; matrix products, arithmetic and copies ran while one was open for 11% of the time, Pallas kernels for 0%

commit v1 on v0

--- a/solution.py
+++ b/solution.py
@@ -151,7 +151,7 @@
         )
         node_total = inner_total + outer_total
         energy_local = inner_energy + outer_energy
-        total_energy = lax.psum(energy_local, ("gx", "gy", "gz"))
+        total_energy = lax.psum(lax.psum(energy_local, ("gy", "gz")), "gx")
         scale_factor = 1.0 / (1.0 + total_energy / (slot_count * devices))
         correction = (
             relax_factor

time: 595 us -> 507 us (0.85)
  blocking collectives: 258 us -> 166 us
    psum x5 -> x10, blocking collectives: 218 us -> 129 us  [local(): total_energy = lax.psum(lax.psum(energy_local, ('gy', 'gz')), 'gx')]
  transfers between devices with their start and end apart: 30 -> 30, of which waited for: 11 -> 14; matrix products, arithmetic and copies ran while one was open for 11% -> 13% of each run, Pallas kernels for 0% -> 0%
where the time goes in v1:
time: 507 us; the launch traced here: 497 us
  blocking collectives  166 us (33%)
  matrix products  107 us (21%)
  starting transfers between devices  84.5 us (17%)
  local copies, waits for them, and re-layouts  78.1 us (15%)
  other arithmetic  38.2 us (8%)
  between operations  12.8 us (3%)
  waiting for transfers between devices  10.4 us (2%)
    psum x10, blocking collectives, local(): total_energy = lax.psum(lax.psum(energy_local, ('gy', 'gz')), 'gx')  129 us
    ppermute x15, starting transfers between devices, extended(): lax.ppermute(tail, axis, [(i, (i + 1) % count) for i in range(ends)])  65.1 us
    psum x1, blocking collectives, local(): residuals.append(lax.psum(residual_local, ('gx', 'gy', 'gz')))  37.8 us
    dot_general x10, matrix products, sweep_add_group(): jnp.einsum('bcn,bpn->bcp', near_lines, near_hot, precision=highest)  29.1 us
    dot_general x15, matrix products, select_lines(): return jnp.einsum('bl,cln->bcn', line_hot, field_lines, precision=highest)  27.3 us
    concatenate x10, other arithmetic, extended(): jnp.concatenate([lax.ppermute(tail, axis, [(i, (i + 1) % count) for i in...  25 us
    ppermute x15, starting transfers between devices, extended(): lax.ppermute(head, axis, [((i + 1) % count, i) for i in range(ends)])  19.4 us
    dot_general x10, matrix products, sweep_add_group(): far_vals = jnp.einsum('bcn,bpn->bcp', far_lines, far_hot, precision=highest)  19.2 us
  transfers between devices with their start and end apart: 30, of which 14 were waited for; matrix products, arithmetic and copies ran while one was open for 13% of the time, Pallas kernels for 0%

profile of v1, /device:TPU:0, one launch (start us, length us, event | category | flops | bytes accessed | tf_op | source)
XLA Modules:
  0.0 497.2 jit_solution(14605163667762116958)
XLA Ops:
  3.7 5.6 %collective-permute-start = (f32[3,3,16,256]{3,1,2,0:T(4,128)S(1)}, f32[3,3,16,256]{3,1,2,0:T(4,128)S(1)}, u32[]{:S(2)}, u32[]{:S(2)}) collective-permute-start(f32[3,3,16,256]{3,1,2,0:T(4,128)S(1)} %get-tuple-element.615), channel_id=1, source_target_pairs={{0,8},{8,16},{16,24},{1,9},{9,17},{17,25},{2,10},{10,18},{18,26},{... | collective-permute-start | bytes 442376 | tf_op jit(solution)/shard_map/ppermute | solution.py:21
  32.9 4.6 collective-permute-start.2
  67.7 17.0 %psum.105 = f32[]{:T(128)} all-reduce(f32[]{:T(128)S(6)} %add.359), channel_id=1, replica_groups=mesh['gx'=4,'gy'=4,'gz'=2] {'gy','gz'}, use_global_device_ids=true, to_apply=%region_2.3 | all-reduce | flops 1 | bytes 8 | tf_op jit(solution)/shard_map/psum | solution.py:154
  85.5 10.7 %psum.106 = f32[]{:T(128)} all-reduce(f32[]{:T(128)} %psum.105), channel_id=1, replica_groups=mesh['gx'=4,'gy'=4,'gz'=2] {'gx'}, use_global_device_ids=true, to_apply=%region_3.4 | all-reduce | flops 1 | bytes 8 | tf_op jit(solution)/shard_map/psum | solution.py:154
  100.6 4.6 collective-permute-start.6
  109.3 4.6 collective-permute-start.8
  133.2 5.1 %pad_maximum_fusion.1 = (f32[3,22,22,262]{3,2,1,0:T(8,128)}, f32[3,22,22,262]{3,2,1,0:T(8,128)}) fusion(f32[3,22,22,3]{3,2,1,0:T(8,128)S(1)} %copy.300, f32[3,22,3,256]{3,2,1,0:T(4,128)S(1)} %copy.296, f32[3,3,16,256]{3,2,1,0:T(8,128)S(1)} %collective-permute-done.7, f32[3,16,16,256]{3,2,1,0:T(8,128)S(1)} %divide_add_fusion.4, ...), kind=kLoop, calls=%fused_computation.50 | loop fusion | flops 2282544 | bytes 4565088 | tf_op jit(solution)/shard_map/concatenate | solution.py:19
  157.0 13.3 %psum.107 = f32[]{:T(128)} all-reduce(f32[]{:T(128)S(6)} %add.369), channel_id=1, replica_groups=mesh['gx'=4,'gy'=4,'gz'=2] {'gy','gz'}, use_global_device_ids=true, to_apply=%region_8.9 | all-reduce | flops 1 | bytes 8 | tf_op jit(solution)/shard_map/psum | solution.py:154
  170.8 11.5 %psum.108 = f32[]{:T(128)} all-reduce(f32[]{:T(128)} %psum.107), channel_id=1, replica_groups=mesh['gx'=4,'gy'=4,'gz'=2] {'gx'}, use_global_device_ids=true, to_apply=%region_9.10 | all-reduce | flops 1 | bytes 8 | tf_op jit(solution)/shard_map/psum | solution.py:154
  186.7 4.6 collective-permute-start.12
  195.4 5.0 collective-permute-start.14
  219.2 5.0 pad_maximum_fusion.2
  243.7 14.3 %psum.109 = f32[]{:T(128)} all-reduce(f32[]{:T(128)S(6)} %add.377), channel_id=1, replica_groups=mesh['gx'=4,'gy'=4,'gz'=2] {'gy','gz'}, use_global_device_ids=true, to_apply=%region_12.13 | all-reduce | flops 1 | bytes 8 | tf_op jit(solution)/shard_map/psum | solution.py:154
  258.6 11.2 %psum.110 = f32[]{:T(128)} all-reduce(f32[]{:T(128)} %psum.109), channel_id=1, replica_groups=mesh['gx'=4,'gy'=4,'gz'=2] {'gx'}, use_global_device_ids=true, to_apply=%region_13.14 | all-reduce | flops 1 | bytes 8 | tf_op jit(solution)/shard_map/psum | solution.py:154
  274.2 4.6 collective-permute-start.18
  283.0 4.6 collective-permute-start.20
  306.8 5.1 %pad_maximum_fusion.3 = (f32[3,22,22,262]{3,2,1,0:T(8,128)}, f32[3,22,22,262]{3,2,1,0:T(8,128)}) fusion(f32[3,22,22,3]{3,2,1,0:T(8,128)S(1)} %copy.352, f32[3,22,3,256]{3,2,1,0:T(4,128)S(1)} %copy.348, f32[3,3,16,256]{3,2,1,0:T(8,128)S(1)} %collective-permute-done.19, f32[3,16,16,256]{3,2,1,0:T(8,128)S(1)} %divide_add_fusion.2, ...), kind=kLoop, calls=%fused_computation.52 | loop fusion | flops 2282544 | bytes 4565088 | tf_op jit(solution)/shard_map/concatenate | solution.py:19
  330.6 13.4 %psum.111 = f32[]{:T(128)} all-reduce(f32[]{:T(128)S(6)} %add.385), channel_id=1, replica_groups=mesh['gx'=4,'gy'=4,'gz'=2] {'gy','gz'}, use_global_device_ids=true, to_apply=%region_16.17 | all-reduce | flops 1 | bytes 8 | tf_op jit(solution)/shard_map/psum | solution.py:154
  344.6 11.1 %psum.112 = f32[]{:T(128)} all-reduce(f32[]{:T(128)} %psum.111), channel_id=1, replica_groups=mesh['gx'=4,'gy'=4,'gz'=2] {'gx'}, use_global_device_ids=true, to_apply=%region_17.18 | all-reduce | flops 1 | bytes 8 | tf_op jit(solution)/shard_map/psum | solution.py:154
  368.9 4.8 collective-permute-start.26
  392.4 5.0 pad_maximum_fusion.4
  418.6 14.8 %psum.113 = f32[]{:T(128)} all-reduce(f32[]{:T(128)S(6)} %add.393), channel_id=1, replica_groups=mesh['gx'=4,'gy'=4,'gz'=2] {'gy','gz'}, use_global_device_ids=true, to_apply=%region_20.21 | all-reduce | flops 1 | bytes 8 | tf_op jit(solution)/shard_map/psum | solution.py:154
  435.7 11.3 %psum.114 = f32[]{:T(128)} all-reduce(f32[]{:T(128)} %psum.113), channel_id=1, replica_groups=mesh['gx'=4,'gy'=4,'gz'=2] {'gx'}, use_global_device_ids=true, to_apply=%region_21.22 | all-reduce | flops 1 | bytes 8 | tf_op jit(solution)/shard_map/psum | solution.py:154
  452.0 37.8 %all-reduce.5 = (f32[1,1]{1,0:T(1,128)}, f32[1,1]{1,0:T(1,128)}, f32[1,1]{1,0:T(1,128)}, f32[1,1]{1,0:T(1,128)}, f32[1,1]{1,0:T(1,128)}) all-reduce(f32[1,1]{1,0:T(1,128)} %bitcast.57, f32[1,1]{1,0:T(1,128)} %bitcast.58, f32[1,1]{1,0:T(1,128)} %bitcast.59, ...), channel_id=1, replica_groups=mesh['gx'=4,'gy'=4,'gz'=2] {'gx','gy','gz'}, use_global_device_ids=true, to_apply=%region_23.24 | all-reduce | flops 5 | bytes 40 | tf_op jit(solution)/shard_map/psum | solution.py:164
  (399 shorter events, 259.5 us)
Async XLA Ops:
  2.4 29.1 %collective-permute-start.1 = (f32[3,3,16,256]{3,1,2,0:T(4,128)S(1)}, f32[3,3,16,256]{3,1,2,0:T(4,128)S(1)}, u32[]{:S(2)}, u32[]{:S(2)}) collective-permute-start(f32[3,3,16,256]{3,1,2,0:T(4,128)S(1)} %get-tuple-element.616), channel_id=1, source_target_pairs={{8,0},{16,8},{24,16},{9,1},{17,9},{25,17},{10,2},{18,10},{26,18},{... | collective-permute-start | bytes 442376 | tf_op jit(solution)/shard_map/ppermute | solution.py:23
  3.7 27.8 %collective-permute-start = (f32[3,3,16,256]{3,1,2,0:T(4,128)S(1)}, f32[3,3,16,256]{3,1,2,0:T(4,128)S(1)}, u32[]{:S(2)}, u32[]{:S(2)}) collective-permute-start(f32[3,3,16,256]{3,1,2,0:T(4,128)S(1)} %get-tuple-element.615), channel_id=1, source_target_pairs={{0,8},{8,16},{16,24},{1,9},{9,17},{17,25},{2,10},{10,18},{18,26},{... | collective-permute-start | bytes 442376 | tf_op jit(solution)/shard_map/ppermute | solution.py:21
  31.6 9.3 %collective-permute-start.3 = (f32[3,22,3,256]{3,1,2,0:T(8,128)S(1)}, f32[3,22,3,256]{3,1,2,0:T(8,128)S(1)}, u32[]{:S(2)}, u32[]{:S(2)}) collective-permute-start(f32[3,22,3,256]{3,1,2,0:T(8,128)S(1)} %get-tuple-element.590), channel_id=1, source_target_pairs={{2,0},{4,2},{6,4},{3,1},{5,3},{7,5},{10,8},{12,10},{14,12},{11,9},... | collective-permute-start | bytes 608264 | tf_op jit(solution)/shard_map/ppermute | solution.py:23
  32.9 8.7 %collective-permute-start.2 = (f32[3,22,3,256]{3,1,2,0:T(8,128)S(1)}, f32[3,22,3,256]{3,1,2,0:T(8,128)S(1)}, u32[]{:S(2)}, u32[]{:S(2)}) collective-permute-start(f32[3,22,3,256]{3,1,2,0:T(8,128)S(1)} %get-tuple-element.589), channel_id=1, source_target_pairs={{0,2},{2,4},{4,6},{1,3},{3,5},{5,7},{8,10},{10,12},{12,14},{9,11},... | collective-permute-start | bytes 608264 | tf_op jit(solution)/shard_map/ppermute | solution.py:21
  46.0 7.8 %collective-permute-start.5 = (f32[3,22,22,3]{2,1,3,0:T(8,128)S(1)}, f32[3,22,22,3]{2,1,3,0:T(8,128)S(1)}, u32[]{:S(2)}, u32[]{:S(2)}) collective-permute-start(f32[3,22,22,3]{2,1,3,0:T(8,128)S(1)} %copy.270), channel_id=1, source_target_pairs={{1,0},{3,2},{5,4},{7,6},{9,8},{11,10},{13,12},{15,14},{17,16},{19,... | collective-permute-start | bytes 52280 | tf_op jit(solution)/shard_map/ppermute | solution.py:23
  100.6 7.2 %collective-permute-start.6 = (f32[3,3,16,256]{3,2,1,0:T(8,128)S(1)}, f32[3,3,16,256]{3,2,1,0:T(8,128)S(1)}, u32[]{:S(2)}, u32[]{:S(2)}) collective-permute-start(f32[3,3,16,256]{3,2,1,0:T(8,128)S(1)} %get-tuple-element.613), channel_id=1, source_target_pairs={{0,8},{8,16},{16,24},{1,9},{9,17},{17,25},{2,10},{10,18},{18,26},{... | collective-permute-start | bytes 442376 | tf_op jit(solution)/shard_map/ppermute | solution.py:21
  108.0 8.1 %collective-permute-start.9 = (f32[3,22,3,256]{3,1,2,0:T(8,128)S(1)}, f32[3,22,3,256]{3,1,2,0:T(8,128)S(1)}, u32[]{:S(2)}, u32[]{:S(2)}) collective-permute-start(f32[3,22,3,256]{3,1,2,0:T(8,128)S(1)} %copy.294), channel_id=1, source_target_pairs={{2,0},{4,2},{6,4},{3,1},{5,3},{7,5},{10,8},{12,10},{14,12},{11,9},... | collective-permute-start | bytes 608264 | tf_op jit(solution)/shard_map/ppermute | solution.py:23
  109.3 8.0 %collective-permute-start.8 = (f32[3,22,3,256]{3,1,2,0:T(8,128)S(1)}, f32[3,22,3,256]{3,1,2,0:T(8,128)S(1)}, u32[]{:S(2)}, u32[]{:S(2)}) collective-permute-start(f32[3,22,3,256]{3,1,2,0:T(8,128)S(1)} %copy.293), channel_id=1, source_target_pairs={{0,2},{2,4},{4,6},{1,3},{3,5},{5,7},{8,10},{10,12},{12,14},{9,11},... | collective-permute-start | bytes 608264 | tf_op jit(solution)/shard_map/ppermute | solution.py:21
  120.8 10.4 %collective-permute-start.11 = (f32[3,22,22,3]{2,1,3,0:T(8,128)S(1)}, f32[3,22,22,3]{2,1,3,0:T(8,128)S(1)}, u32[]{:S(2)}, u32[]{:S(2)}) collective-permute-start(f32[3,22,22,3]{2,1,3,0:T(8,128)S(1)} %copy.298), channel_id=1, source_target_pairs={{1,0},{3,2},{5,4},{7,6},{9,8},{11,10},{13,12},{15,14},{17,16},{19,... | collective-permute-start | bytes 52280 | tf_op jit(solution)/shard_map/ppermute | solution.py:23
  123.8 8.0 %collective-permute-start.10 = (f32[3,22,22,3]{2,1,3,0:T(8,128)S(1)}, f32[3,22,22,3]{2,1,3,0:T(8,128)}, u32[]{:S(2)}, u32[]{:S(2)}) collective-permute-start(f32[3,22,22,3]{2,1,3,0:T(8,128)S(1)} %copy.297), channel_id=1, source_target_pairs={{0,1},{2,3},{4,5},{6,7},{8,9},{10,11},{12,13},{14,15},{16,17},{18,... | collective-permute-start | bytes 52280 | tf_op jit(solution)/shard_map/ppermute | solution.py:21
  194.1 9.1 %collective-permute-start.15 = (f32[3,22,3,256]{3,1,2,0:T(8,128)S(1)}, f32[3,22,3,256]{3,1,2,0:T(8,128)S(1)}, u32[]{:S(2)}, u32[]{:S(2)}) collective-permute-start(f32[3,22,3,256]{3,1,2,0:T(8,128)S(1)} %copy.320), channel_id=1, source_target_pairs={{2,0},{4,2},{6,4},{3,1},{5,3},{7,5},{10,8},{12,10},{14,12},{11,9},... | collective-permute-start | bytes 608264 | tf_op jit(solution)/shard_map/ppermute | solution.py:23
  195.4 8.0 %collective-permute-start.14 = (f32[3,22,3,256]{3,1,2,0:T(8,128)S(1)}, f32[3,22,3,256]{3,1,2,0:T(8,128)S(1)}, u32[]{:S(2)}, u32[]{:S(2)}) collective-permute-start(f32[3,22,3,256]{3,1,2,0:T(8,128)S(1)} %copy.319), channel_id=1, source_target_pairs={{0,2},{2,4},{4,6},{1,3},{3,5},{5,7},{8,10},{10,12},{12,14},{9,11},... | collective-permute-start | bytes 608264 | tf_op jit(solution)/shard_map/ppermute | solution.py:21
  207.9 8.5 %collective-permute-start.17 = (f32[3,22,22,3]{2,1,3,0:T(8,128)S(1)}, f32[3,22,22,3]{2,1,3,0:T(8,128)S(1)}, u32[]{:S(2)}, u32[]{:S(2)}) collective-permute-start(f32[3,22,22,3]{2,1,3,0:T(8,128)S(1)} %copy.324), channel_id=1, source_target_pairs={{1,0},{3,2},{5,4},{7,6},{9,8},{11,10},{13,12},{15,14},{17,16},{19,... | collective-permute-start | bytes 52280 | tf_op jit(solution)/shard_map/ppermute | solution.py:23
  209.7 8.0 %collective-permute-start.16 = (f32[3,22,22,3]{2,1,3,0:T(8,128)S(1)}, f32[3,22,22,3]{2,1,3,0:T(8,128)S(1)}, u32[]{:S(2)}, u32[]{:S(2)}) collective-permute-start(f32[3,22,22,3]{2,1,3,0:T(8,128)S(1)} %copy.323), channel_id=1, source_target_pairs={{0,1},{2,3},{4,5},{6,7},{8,9},{10,11},{12,13},{14,15},{16,17},{18,... | collective-permute-start | bytes 52280 | tf_op jit(solution)/shard_map/ppermute | solution.py:21
  274.2 7.2 %collective-permute-start.18 = (f32[3,3,16,256]{3,2,1,0:T(8,128)S(1)}, f32[3,3,16,256]{3,2,1,0:T(8,128)S(1)}, u32[]{:S(2)}, u32[]{:S(2)}) collective-permute-start(f32[3,3,16,256]{3,2,1,0:T(8,128)S(1)} %get-tuple-element.605), channel_id=1, source_target_pairs={{0,8},{8,16},{16,24},{1,9},{9,17},{17,25},{2,10},{10,18},{18,26},{... | collective-permute-start | bytes 442376 | tf_op jit(solution)/shard_map/ppermute | solution.py:21
  281.6 8.1 %collective-permute-start.21 = (f32[3,22,3,256]{3,1,2,0:T(8,128)S(1)}, f32[3,22,3,256]{3,1,2,0:T(8,128)S(1)}, u32[]{:S(2)}, u32[]{:S(2)}) collective-permute-start(f32[3,22,3,256]{3,1,2,0:T(8,128)S(1)} %copy.346), channel_id=1, source_target_pairs={{2,0},{4,2},{6,4},{3,1},{5,3},{7,5},{10,8},{12,10},{14,12},{11,9},... | collective-permute-start | bytes 608264 | tf_op jit(solution)/shard_map/ppermute | solution.py:23
  283.0 8.0 %collective-permute-start.20 = (f32[3,22,3,256]{3,1,2,0:T(8,128)S(1)}, f32[3,22,3,256]{3,1,2,0:T(8,128)S(1)}, u32[]{:S(2)}, u32[]{:S(2)}) collective-permute-start(f32[3,22,3,256]{3,1,2,0:T(8,128)S(1)} %copy.345), channel_id=1, source_target_pairs={{0,2},{2,4},{4,6},{1,3},{3,5},{5,7},{8,10},{10,12},{12,14},{9,11},... | collective-permute-start | bytes 608264 | tf_op jit(solution)/shard_map/ppermute | solution.py:21
  294.5 10.4 %collective-permute-start.23 = (f32[3,22,22,3]{2,1,3,0:T(8,128)S(1)}, f32[3,22,22,3]{2,1,3,0:T(8,128)S(1)}, u32[]{:S(2)}, u32[]{:S(2)}) collective-permute-start(f32[3,22,22,3]{2,1,3,0:T(8,128)S(1)} %copy.350), channel_id=1, source_target_pairs={{1,0},{3,2},{5,4},{7,6},{9,8},{11,10},{13,12},{15,14},{17,16},{19,... | collective-permute-start | bytes 52280 | tf_op jit(solution)/shard_map/ppermute | solution.py:23
  297.4 7.9 %collective-permute-start.22 = (f32[3,22,22,3]{2,1,3,0:T(8,128)S(1)}, f32[3,22,22,3]{2,1,3,0:T(8,128)}, u32[]{:S(2)}, u32[]{:S(2)}) collective-permute-start(f32[3,22,22,3]{2,1,3,0:T(8,128)S(1)} %copy.349), channel_id=1, source_target_pairs={{0,1},{2,3},{4,5},{6,7},{8,9},{10,11},{12,13},{14,15},{16,17},{18,... | collective-permute-start | bytes 52280 | tf_op jit(solution)/shard_map/ppermute | solution.py:21
  360.2 7.2 %collective-permute-start.24 = (f32[3,3,16,256]{3,2,1,0:T(8,128)S(1)}, f32[3,3,16,256]{3,2,1,0:T(8,128)S(1)}, u32[]{:S(2)}, u32[]{:S(2)}) collective-permute-start(f32[3,3,16,256]{3,2,1,0:T(8,128)S(1)} %get-tuple-element.601), channel_id=1, source_target_pairs={{0,8},{8,16},{16,24},{1,9},{9,17},{17,25},{2,10},{10,18},{18,26},{... | collective-permute-start | bytes 442376 | tf_op jit(solution)/shard_map/ppermute | solution.py:21
  367.5 8.9 %collective-permute-start.27 = (f32[3,22,3,256]{3,1,2,0:T(8,128)S(1)}, f32[3,22,3,256]{3,1,2,0:T(8,128)S(1)}, u32[]{:S(2)}, u32[]{:S(2)}) collective-permute-start(f32[3,22,3,256]{3,1,2,0:T(8,128)S(1)} %copy.372), channel_id=1, source_target_pairs={{2,0},{4,2},{6,4},{3,1},{5,3},{7,5},{10,8},{12,10},{14,12},{11,9},... | collective-permute-start | bytes 608264 | tf_op jit(solution)/shard_map/ppermute | solution.py:23
  368.9 8.0 %collective-permute-start.26 = (f32[3,22,3,256]{3,1,2,0:T(8,128)S(1)}, f32[3,22,3,256]{3,1,2,0:T(8,128)S(1)}, u32[]{:S(2)}, u32[]{:S(2)}) collective-permute-start(f32[3,22,3,256]{3,1,2,0:T(8,128)S(1)} %copy.371), channel_id=1, source_target_pairs={{0,2},{2,4},{4,6},{1,3},{3,5},{5,7},{8,10},{10,12},{12,14},{9,11},... | collective-permute-start | bytes 608264 | tf_op jit(solution)/shard_map/ppermute | solution.py:21
  381.1 8.5 %collective-permute-start.29 = (f32[3,22,22,3]{2,1,3,0:T(8,128)S(1)}, f32[3,22,22,3]{2,1,3,0:T(8,128)S(1)}, u32[]{:S(2)}, u32[]{:S(2)}) collective-permute-start(f32[3,22,22,3]{2,1,3,0:T(8,128)S(1)} %copy.376), channel_id=1, source_target_pairs={{1,0},{3,2},{5,4},{7,6},{9,8},{11,10},{13,12},{15,14},{17,16},{19,... | collective-permute-start | bytes 52280 | tf_op jit(solution)/shard_map/ppermute | solution.py:23
  383.0 8.0 %collective-permute-start.28 = (f32[3,22,22,3]{2,1,3,0:T(8,128)S(1)}, f32[3,22,22,3]{2,1,3,0:T(8,128)S(1)}, u32[]{:S(2)}, u32[]{:S(2)}) collective-permute-start(f32[3,22,22,3]{2,1,3,0:T(8,128)S(1)} %copy.375), channel_id=1, source_target_pairs={{0,1},{2,3},{4,5},{6,7},{8,9},{10,11},{12,13},{14,15},{16,17},{18,... | collective-permute-start | bytes 52280 | tf_op jit(solution)/shard_map/ppermute | solution.py:21
  (77 other events, 861.1 us)
